TPU v7x, 256 devices: a whole 4x4x8 slice. The times are simulated.
256 devices in a mesh: gx: 16 (over z, core), gy: 4 (over y), gz: 4 (over x).
Axes of the slice: x: 4, y: 4, z: 8, core: 2. Of those that a mesh axis runs over, the one named last changes fastest.
Arguments:
- queries: bfloat16 [128, 32, 128], P(None, 'gy'), may hold values from -6 to 6
- passages: bfloat16 [8192, 256, 128], P('gx', 'gz'), may hold values from -0.5 to 0.5
- passage_len: int32 [8192], P('gx'), may hold values from 32 to 256
- query_len: int32 [128], replicated, may hold values from 8 to 32
Outputs:
- log_probs: float32 [128, 8192], P(None, ('gx', 'gz'))
All inputs are finite; a program needn't handle non-finite values.
Results may differ from a plain program's by a relative error of at most 0.0003.
Values sent between devices are 32-bit elements; how exact they have to be, the bound alone decides.
A program may use at most 64 MiB of HBM per device.

v0:
```python
import math

import jax
import jax.numpy as jnp
from jax import lax
from jax.sharding import PartitionSpec as P

masked_low = -1e30


def copy_for_each(array, axis):
    devices = lax.axis_size(axis)
    return lax.all_to_all(
        jnp.broadcast_to(array[None], (devices, *array.shape)), axis, 0, 0, tiled=True
    )


def taken_together(array, axis):
    return copy_for_each(array, axis).sum(axis=0)


def collected_together(array, axis):
    leaves = jax.tree.leaves(array)
    order = sorted(range(len(leaves)), key=lambda k: -leaves[k].size)
    width = (1, *leaves[order[0]].shape)[-1]
    lines = [
        jnp.pad(leaves[k].reshape(-1), (0, -leaves[k].size % width)).reshape(-1, width)
        for k in order
    ]
    both, at, found = (copy_for_each(jnp.concatenate(lines), axis), 0, {})
    for k, line in zip(order, lines):
        section = both[:, at : at + len(line)].reshape(len(both), -1)
        found[k] = section[:, : leaves[k].size].reshape(-1, *leaves[k].shape)
        at += len(line)
    numbers = iter(range(len(leaves)))
    return jax.tree.map(lambda _: found[next(numbers)], array)


def joined_by_halves(pieces, combine):
    while len(jax.tree.leaves(pieces)[0]) > 1:
        pieces = jax.vmap(combine)(
            *(jax.tree.map(lambda part: part[side::2], pieces) for side in (0, 1))
        )
    return jax.tree.map(lambda part: part[0], pieces)


def joined_all(array, axis, combine):
    pieces = collected_together(array, axis)
    return joined_by_halves(pieces, combine)


def token_maxima(queries, passages, passage_len):
    query_count = queries.shape[0]
    query_rows = queries.shape[1]
    width = queries.shape[2]
    passage_count = passages.shape[0]
    token_count = passages.shape[1]
    flat_queries = queries.reshape(query_count * query_rows, width)
    per_block = math.gcd(passage_count, 32)
    num_blocks = passage_count // per_block
    token_ids = lax.axis_index("gz") * token_count + jnp.arange(token_count, dtype=jnp.int32)
    tile_stack = passages.reshape(num_blocks, per_block * token_count, width)
    length_stack = passage_len.reshape(num_blocks, per_block)

    def block_maxima(packed):
        passage_tile, tile_len = packed
        scores = lax.dot_general(
            flat_queries, passage_tile, (((1,), (1,)), ((), ())), preferred_element_type=jnp.float32
        )
        scores = scores.reshape(query_count * query_rows, per_block, token_count)
        usable = token_ids[None, :] < tile_len[:, None]
        scores = jnp.where(usable[None], scores, masked_low)
        return jnp.max(scores, axis=2)

    pieces = lax.map(block_maxima, (tile_stack, length_stack))
    return jnp.transpose(pieces, (1, 0, 2)).reshape(query_count, query_rows, passage_count)


def join_pairs(earlier, other_pair):
    highest = jnp.maximum(earlier[0], other_pair[0])
    summed = earlier[1] * jnp.exp(earlier[0] - highest) + other_pair[1] * jnp.exp(
        other_pair[0] - highest
    )
    return (highest, summed)


def fold_peers(received):
    return jnp.max(received, axis=2)


def shards(queries, passages, passage_len, query_len):
    maxima = token_maxima(queries, passages, passage_len)
    query_count = maxima.shape[0]
    query_rows = maxima.shape[1]
    passage_count = maxima.shape[2]
    query_ids = lax.axis_index("gy") * query_rows + jnp.arange(query_rows, dtype=jnp.int32)
    counted = (query_ids[None, :] < query_len[:, None])[:, :, None]
    spread = maxima.reshape(query_count, query_rows, 1, passage_count)
    merged = fold_peers(lax.all_to_all(spread, "gz", split_axis=3, concat_axis=2, tiled=True))
    partial_value = jnp.sum(jnp.where(counted, merged, 0.0), axis=1)
    scores_here = taken_together(partial_value, "gy")
    local_top = jnp.max(scores_here, axis=1)
    local_sum = jnp.sum(jnp.exp(scores_here - local_top[:, None]), axis=1)
    highest, summed = joined_all((local_top, local_sum), ("gx", "gz"), join_pairs)
    return scores_here - (highest + jnp.log(summed))[:, None]


def solution(mesh):
    return jax.shard_map(
        shards,
        mesh=mesh,
        in_specs=(P(None, "gy", None), P("gx", "gz", None), P("gx"), P()),
        out_specs=P(None, ("gx", "gz")),
        check_vma=False,
    )
```

profile of v0, /device:TPU:1, one launch (start us, length us, event | category | flops | bytes accessed | tf_op | source)
XLA Modules:
  0.0 130.1 jit_solution(9524589594752104741)
XLA Ops:
  0.8 40.5 %while.11 = (s32[]{:T(128)}, f32[16,1024,32]{1,2,0:T(8,128)S(1)}, s32[16,32]{1,0:T(8,128)S(1)}, bf16[16,2048,128]{2,1,0:T(8,128)(2,1)}, bf16[1024,128]{1,0:T(8,128)(2,1)}, /*index=5*/s32[]{:T(128)}, s32[]{:T(128)}) while((s32[]{:T(128)}, f32[16,1024,32]{1,2,0:T(8,128)S(1)}, s32[16,32]{1,0:T(8,128)S(1)}, ...), condition=%wide.region_2.3_spmd.clone, body=%wide.region_0.2_spmd.clone.sunk | while | flops 541034560 | bytes 1185241 | solution.py:75
  0.8 2.4 %select_reduce_fusion.3 = f32[1024,32]{0,1:T(8,128)S(1)} fusion(pred[32,64]{1,0:T(8,128)(4,1)S(1)} %broadcast_compare_fusion.3, bf16[1024,128]{1,0:T(8,128)(2,1)} %get-tuple-element.132, bf16[16,2048,128]{2,1,0:T(8,128)(2,1)} %get-tuple-element.131, s32[]{:T(128)} %get-tuple-element.121), kind=kOutput, calls=%fused_computation.1.clone.1 | convolution fusion | flops 541032448 | bytes 920064 | tf_op jit(solution)/shard_map/while/body/eval_jaxpr/dot_general | solution.py:67
  3.4 2.4 %select_reduce_fusion.3 = f32[1024,32]{0,1:T(8,128)S(1)} fusion(pred[32,64]{1,0:T(8,128)(4,1)S(1)} %broadcast_compare_fusion.3, bf16[1024,128]{1,0:T(8,128)(2,1)} %get-tuple-element.132, bf16[16,2048,128]{2,1,0:T(8,128)(2,1)} %get-tuple-element.131, s32[]{:T(128)} %get-tuple-element.121), kind=kOutput, calls=%fused_computation.1.clone.1 | convolution fusion | flops 541032448 | bytes 920064 | tf_op jit(solution)/shard_map/while/body/eval_jaxpr/dot_general | solution.py:67
  5.9 2.4 %select_reduce_fusion.3 = f32[1024,32]{0,1:T(8,128)S(1)} fusion(pred[32,64]{1,0:T(8,128)(4,1)S(1)} %broadcast_compare_fusion.3, bf16[1024,128]{1,0:T(8,128)(2,1)} %get-tuple-element.132, bf16[16,2048,128]{2,1,0:T(8,128)(2,1)} %get-tuple-element.131, s32[]{:T(128)} %get-tuple-element.121), kind=kOutput, calls=%fused_computation.1.clone.1 | convolution fusion | flops 541032448 | bytes 920064 | tf_op jit(solution)/shard_map/while/body/eval_jaxpr/dot_general | solution.py:67
  8.4 2.4 %select_reduce_fusion.3 = f32[1024,32]{0,1:T(8,128)S(1)} fusion(pred[32,64]{1,0:T(8,128)(4,1)S(1)} %broadcast_compare_fusion.3, bf16[1024,128]{1,0:T(8,128)(2,1)} %get-tuple-element.132, bf16[16,2048,128]{2,1,0:T(8,128)(2,1)} %get-tuple-element.131, s32[]{:T(128)} %get-tuple-element.121), kind=kOutput, calls=%fused_computation.1.clone.1 | convolution fusion | flops 541032448 | bytes 920064 | tf_op jit(solution)/shard_map/while/body/eval_jaxpr/dot_general | solution.py:67
  11.0 2.4 %select_reduce_fusion.3 = f32[1024,32]{0,1:T(8,128)S(1)} fusion(pred[32,64]{1,0:T(8,128)(4,1)S(1)} %broadcast_compare_fusion.3, bf16[1024,128]{1,0:T(8,128)(2,1)} %get-tuple-element.132, bf16[16,2048,128]{2,1,0:T(8,128)(2,1)} %get-tuple-element.131, s32[]{:T(128)} %get-tuple-element.121), kind=kOutput, calls=%fused_computation.1.clone.1 | convolution fusion | flops 541032448 | bytes 920064 | tf_op jit(solution)/shard_map/while/body/eval_jaxpr/dot_general | solution.py:67
  13.5 2.4 %select_reduce_fusion.3 = f32[1024,32]{0,1:T(8,128)S(1)} fusion(pred[32,64]{1,0:T(8,128)(4,1)S(1)} %broadcast_compare_fusion.3, bf16[1024,128]{1,0:T(8,128)(2,1)} %get-tuple-element.132, bf16[16,2048,128]{2,1,0:T(8,128)(2,1)} %get-tuple-element.131, s32[]{:T(128)} %get-tuple-element.121), kind=kOutput, calls=%fused_computation.1.clone.1 | convolution fusion | flops 541032448 | bytes 920064 | tf_op jit(solution)/shard_map/while/body/eval_jaxpr/dot_general | solution.py:67
  16.1 2.4 %select_reduce_fusion.3 = f32[1024,32]{0,1:T(8,128)S(1)} fusion(pred[32,64]{1,0:T(8,128)(4,1)S(1)} %broadcast_compare_fusion.3, bf16[1024,128]{1,0:T(8,128)(2,1)} %get-tuple-element.132, bf16[16,2048,128]{2,1,0:T(8,128)(2,1)} %get-tuple-element.131, s32[]{:T(128)} %get-tuple-element.121), kind=kOutput, calls=%fused_computation.1.clone.1 | convolution fusion | flops 541032448 | bytes 920064 | tf_op jit(solution)/shard_map/while/body/eval_jaxpr/dot_general | solution.py:67
  18.6 2.4 %select_reduce_fusion.3 = f32[1024,32]{0,1:T(8,128)S(1)} fusion(pred[32,64]{1,0:T(8,128)(4,1)S(1)} %broadcast_compare_fusion.3, bf16[1024,128]{1,0:T(8,128)(2,1)} %get-tuple-element.132, bf16[16,2048,128]{2,1,0:T(8,128)(2,1)} %get-tuple-element.131, s32[]{:T(128)} %get-tuple-element.121), kind=kOutput, calls=%fused_computation.1.clone.1 | convolution fusion | flops 541032448 | bytes 920064 | tf_op jit(solution)/shard_map/while/body/eval_jaxpr/dot_general | solution.py:67
  21.1 2.4 %select_reduce_fusion.3 = f32[1024,32]{0,1:T(8,128)S(1)} fusion(pred[32,64]{1,0:T(8,128)(4,1)S(1)} %broadcast_compare_fusion.3, bf16[1024,128]{1,0:T(8,128)(2,1)} %get-tuple-element.132, bf16[16,2048,128]{2,1,0:T(8,128)(2,1)} %get-tuple-element.131, s32[]{:T(128)} %get-tuple-element.121), kind=kOutput, calls=%fused_computation.1.clone.1 | convolution fusion | flops 541032448 | bytes 920064 | tf_op jit(solution)/shard_map/while/body/eval_jaxpr/dot_general | solution.py:67
  23.7 2.4 %select_reduce_fusion.3 = f32[1024,32]{0,1:T(8,128)S(1)} fusion(pred[32,64]{1,0:T(8,128)(4,1)S(1)} %broadcast_compare_fusion.3, bf16[1024,128]{1,0:T(8,128)(2,1)} %get-tuple-element.132, bf16[16,2048,128]{2,1,0:T(8,128)(2,1)} %get-tuple-element.131, s32[]{:T(128)} %get-tuple-element.121), kind=kOutput, calls=%fused_computation.1.clone.1 | convolution fusion | flops 541032448 | bytes 920064 | tf_op jit(solution)/shard_map/while/body/eval_jaxpr/dot_general | solution.py:67
  26.2 2.4 %select_reduce_fusion.3 = f32[1024,32]{0,1:T(8,128)S(1)} fusion(pred[32,64]{1,0:T(8,128)(4,1)S(1)} %broadcast_compare_fusion.3, bf16[1024,128]{1,0:T(8,128)(2,1)} %get-tuple-element.132, bf16[16,2048,128]{2,1,0:T(8,128)(2,1)} %get-tuple-element.131, s32[]{:T(128)} %get-tuple-element.121), kind=kOutput, calls=%fused_computation.1.clone.1 | convolution fusion | flops 541032448 | bytes 920064 | tf_op jit(solution)/shard_map/while/body/eval_jaxpr/dot_general | solution.py:67
  28.7 2.4 %select_reduce_fusion.3 = f32[1024,32]{0,1:T(8,128)S(1)} fusion(pred[32,64]{1,0:T(8,128)(4,1)S(1)} %broadcast_compare_fusion.3, bf16[1024,128]{1,0:T(8,128)(2,1)} %get-tuple-element.132, bf16[16,2048,128]{2,1,0:T(8,128)(2,1)} %get-tuple-element.131, s32[]{:T(128)} %get-tuple-element.121), kind=kOutput, calls=%fused_computation.1.clone.1 | convolution fusion | flops 541032448 | bytes 920064 | tf_op jit(solution)/shard_map/while/body/eval_jaxpr/dot_general | solution.py:67
  31.3 2.4 %select_reduce_fusion.3 = f32[1024,32]{0,1:T(8,128)S(1)} fusion(pred[32,64]{1,0:T(8,128)(4,1)S(1)} %broadcast_compare_fusion.3, bf16[1024,128]{1,0:T(8,128)(2,1)} %get-tuple-element.132, bf16[16,2048,128]{2,1,0:T(8,128)(2,1)} %get-tuple-element.131, s32[]{:T(128)} %get-tuple-element.121), kind=kOutput, calls=%fused_computation.1.clone.1 | convolution fusion | flops 541032448 | bytes 920064 | tf_op jit(solution)/shard_map/while/body/eval_jaxpr/dot_general | solution.py:67
  33.8 2.4 %select_reduce_fusion.3 = f32[1024,32]{0,1:T(8,128)S(1)} fusion(pred[32,64]{1,0:T(8,128)(4,1)S(1)} %broadcast_compare_fusion.3, bf16[1024,128]{1,0:T(8,128)(2,1)} %get-tuple-element.132, bf16[16,2048,128]{2,1,0:T(8,128)(2,1)} %get-tuple-element.131, s32[]{:T(128)} %get-tuple-element.121), kind=kOutput, calls=%fused_computation.1.clone.1 | convolution fusion | flops 541032448 | bytes 920064 | tf_op jit(solution)/shard_map/while/body/eval_jaxpr/dot_general | solution.py:67
  38.9 2.4 %select_reduce_fusion.3 = f32[1024,32]{0,1:T(8,128)S(1)} fusion(pred[32,64]{1,0:T(8,128)(4,1)S(1)} %broadcast_compare_fusion.3, bf16[1024,128]{1,0:T(8,128)(2,1)} %get-tuple-element.132, bf16[16,2048,128]{2,1,0:T(8,128)(2,1)} %get-tuple-element.131, s32[]{:T(128)} %get-tuple-element.121), kind=kOutput, calls=%fused_computation.1.clone.1 | convolution fusion | flops 541032448 | bytes 920064 | tf_op jit(solution)/shard_map/while/body/eval_jaxpr/dot_general | solution.py:67
  41.3 6.2 %copy.18 = f32[1024,16,32]{2,1,0:T(8,128)} copy(f32[1024,16,32]{0,2,1:T(8,128)S(1)} %bitcast.37) | data formatting | bytes 4194304 | tf_op jit(solution)/shard_map/transpose | solution.py:76
  47.5 6.2 %reshape_reshape.3 = f32[128,8,1,512]{3,1,0,2:T(8,128)S(1)} reshape(f32[1024,16,32]{2,1,0:T(8,128)} %copy.18) | data formatting | bytes 4194304 | tf_op jit(solution)/shard_map/reshape;reshape | solution.py:98
  55.9 5.0 %all-to-all-start = ((f32[128,8,1,512]{0,1,2,3:T(8,128)}), f32[128,8,1,512]{0,1,2,3:T(8,128)S(1)}, u32[]{:S(2)}, u32[]{:S(2)}) async-start(f32[128,8,1,512]{0,1,2,3:T(8,128)} %copy.19), calls=%async_computation | async-start | bytes 4194304 | tf_op jit(solution)/shard_map/all_to_all | solution.py:99
  60.9 24.4 %all-to-all-done = f32[128,8,1,512]{0,1,2,3:T(8,128)S(1)} async-done(((f32[128,8,1,512]{0,1,2,3:T(8,128)}), f32[128,8,1,512]{0,1,2,3:T(8,128)S(1)}, u32[]{:S(2)}, u32[]{:S(2)}) %all-to-all-start) | async-done | bytes 2097184 | tf_op jit(solution)/shard_map/all_to_all | solution.py:99
  85.5 4.8 %copy.23 = f32[128,8,128]{1,0,2:T(8,128)} copy(f32[128,8,128]{0,1,2:T(8,128)S(1)} %reduce_max.27) | data formatting | bytes 1048576
  90.3 5.6 %select_reduce_fusion.1 = f32[128,128]{0,1:T(8,128)S(1)} fusion(f32[128,8,128]{1,0,2:T(8,128)} %copy.23, pred[128,8]{1,0:T(8,128)(4,1)S(1)} %broadcast_compare_fusion.1), kind=kLoop, calls=%fused_computation.11 | loop fusion | flops 245760 | bytes 590848 | tf_op jit(solution)/shard_map/reduce_sum | solution.py:100
  96.1 10.5 %all_to_all.22 = f32[4,128,128]{2,1,0:T(8,128)S(1)} all-to-all(f32[4,128,128]{2,1,0:T(8,128)S(1)} %broadcast_in_dim.54), channel_id=1, replica_groups=mesh['gx'=16,'gy'=4,'gz'=4] {'gy'}, dimensions={0} | all-to-all | bytes 524288 | tf_op jit(solution)/shard_map/all_to_all | solution.py:13
  107.0 21.9 %all_to_all.23 = f32[64,2,128]{2,1,0:T(2,128)S(1)} all-to-all(f32[64,2,128]{2,1,0:T(2,128)S(1)} %broadcast_in_dim.55), channel_id=1, replica_groups=mesh['gx'=16,'gy'=4,'gz'=4] {'gx','gz'}, dimensions={0} | all-to-all | bytes 131072 | tf_op jit(solution)/shard_map/all_to_all | solution.py:13
  (108 shorter events, 8.8 us)
Async XLA Ops:
  55.9 5.0 %copy-start = (s32[128]{0:T(128)S(1)}, s32[128]{0:T(128)}, u32[]{:S(2)}) copy-start(s32[128]{0:T(128)} %param.9) | copy-start | bytes 1540
  55.9 29.4 %all-to-all-start = ((f32[128,8,1,512]{0,1,2,3:T(8,128)}), f32[128,8,1,512]{0,1,2,3:T(8,128)S(1)}, u32[]{:S(2)}, u32[]{:S(2)}) async-start(f32[128,8,1,512]{0,1,2,3:T(8,128)} %copy.19), calls=%async_computation | async-start | bytes 4194304 | tf_op jit(solution)/shard_map/all_to_all | solution.py:99
where the time goes:
time: 131 us; the launch traced here: 130 us
  matrix products  38.2 us (29%)
  blocking collectives  32.5 us (25%)
  waiting for transfers between devices  24.4 us (19%)
  local copies, waits for them, and re-layouts  21 us (16%)
  other arithmetic  8.28 us (6%)
  starting transfers between devices  4.96 us (4%)
    dot_general x16, matrix products, block_maxima(): lax.dot_general(flat_queries, passage_tile, (((1,), (1,)), ((), ())), pre...  38.2 us
    all_to_all x2, blocking collectives, copy_for_each(): lax.all_to_all(jnp.broadcast_to(array[None], (devices, *array.shape)), ax...  32.5 us
    all_to_all x1, waiting for transfers between devices, shards(): lax.all_to_all(spread, 'gz', split_axis=3, concat_axis=2, tiled=True)  24.4 us
    another operation x2, local copies, waits for them, and re-layouts, shards(): spread = maxima.reshape(query_count, query_rows, 1, passage_count)  8.32 us
    transpose x1, local copies, waits for them, and re-layouts, token_maxima(): jnp.transpose(pieces, (1, 0, 2))  6.23 us
    reduce_sum x1, other arithmetic, shards(): partial_value = jnp.sum(jnp.where(counted, merged, 0.0), axis=1)  5.61 us
    all_to_all x1, starting transfers between devices, shards(): lax.all_to_all(spread, 'gz', split_axis=3, concat_axis=2, tiled=True)  4.96 us
    unnamed x3, local copies, waits for them, and re-layouts  4.83 us
  transfers between devices with their start and end apart: 1, of which 1 were waited for; matrix products, arithmetic and copies ran while one was open for 0% of the time, Pallas kernels for 0%

commit v1 on v0

v1 whole, which is shorter than its diff:
```python
import jax
import jax.numpy as jnp
from jax import lax
from jax.experimental import pallas as pl
from jax.experimental.pallas import tpu as pltpu
from jax.sharding import PartitionSpec as P

masked_low = -1e30
MESH = pl.DeviceIdType.MESH

CHUNK = 32
SHARE = 4
ROWS = 8
TILE = 256


def place(step):
    far, near = (step % 2) * 2 + (step // 2) % 2, step - SHARE
    way, joined, turn = near % 2, (near // 2) % 2, near // 4
    near_piece = turn + 2 * ((way + joined + 1) % 2)
    is_near = jnp.logical_and(step >= SHARE, step < 3 * SHARE)
    offset = jnp.where(step < SHARE, 2, jnp.where(is_near, 1 + 2 * way, 0))
    return offset, jnp.where(is_near, near_piece, far)


def body(
    length_ref, query_ref, count_ref, passages_ref, out_ref,
    held, usable, weights, wide, parts, relay, final, sums, near_stat, far_stat,
    load_sem, relay_sem, final_sem, sums_sem, near_sem, far_sem,
):
    gx, gy, gz = lax.axis_index("gx"), lax.axis_index("gy"), lax.axis_index("gz")
    steps = 4 * SHARE
    tokens, width = passages_ref.shape[1:]
    queries = query_ref.shape[0]

    def load(step):
        offset, piece = place(step)
        start = lax.rem(gz + offset, 4) * (SHARE * CHUNK) + piece * CHUNK
        return pltpu.make_async_copy(
            passages_ref.at[pl.ds(start, CHUNK)], held.at[step], load_sem.at[step]
        )

    for step in range(steps):
        load(jnp.int32(step)).start()

    barrier = pltpu.get_barrier_semaphore()
    for axis, size, here in (("gz", 4, gz), ("gy", 4, gy), ("gx", 16, gx)):
        for k in range(1, size):
            pl.semaphore_signal(
                barrier, inc=1, device_id={axis: lax.rem(here + k, size)}, device_id_type=MESH
            )

    wide[...] = query_ref[...].reshape(queries * ROWS, width).astype(jnp.float32)
    for i in range(ROWS):
        row = wide[pl.ds(i, queries, stride=ROWS), :]
        weights[:, i * queries : (i + 1) * queries] = row.T.astype(jnp.bfloat16)

    sublane = lax.broadcasted_iota(jnp.int32, (8, TILE), 0)
    odd = [(sublane & k) != 0 for k in (1, 2, 4)]
    token = lax.broadcasted_iota(jnp.int32, (tokens, width), 0)

    def relay_copy(way, turn, source):
        return pltpu.make_async_remote_copy(
            src_ref=source, dst_ref=relay.at[way, turn],
            send_sem=relay_sem.at[0, way, turn], recv_sem=relay_sem.at[1, way, turn],
            device_id={"gz": lax.rem(gz + 1 + 2 * way, 4)}, device_id_type=MESH,
        )

    def final_copy(way, piece, source):
        return pltpu.make_async_remote_copy(
            src_ref=source, dst_ref=final.at[way, piece],
            send_sem=final_sem.at[0, way, piece], recv_sem=final_sem.at[1, way, piece],
            device_id={"gz": lax.rem(gz + 1 + 2 * way, 4)}, device_id_type=MESH,
        )

    def sums_copy(k, piece):
        return pltpu.make_async_remote_copy(
            src_ref=sums.at[gy, piece], dst_ref=sums.at[gy, piece],
            send_sem=sums_sem.at[0, k, piece], recv_sem=sums_sem.at[1, k, piece],
            device_id={"gy": lax.rem(gy + k, 4)}, device_id_type=MESH,
        )

    def near_copy(k):
        return pltpu.make_async_remote_copy(
            src_ref=near_stat.at[gz], dst_ref=near_stat.at[gz],
            send_sem=near_sem.at[0, k], recv_sem=near_sem.at[1, k],
            device_id={"gz": lax.rem(gz + k, 4)}, device_id_type=MESH,
        )

    def far_copy(k):
        return pltpu.make_async_remote_copy(
            src_ref=far_stat.at[gx], dst_ref=far_stat.at[gx],
            send_sem=far_sem.at[0, k], recv_sem=far_sem.at[1, k],
            device_id={"gx": lax.rem(gx + k, 16)}, device_id_type=MESH,
        )

    def score(step):
        offset, piece = place(step)
        start = lax.rem(gz + offset, 4) * (SHARE * CHUNK) + piece * CHUNK
        load(step).wait()
        for half in range(CHUNK // 8):
            some = jnp.zeros((8, TILE), jnp.int32)
            for p in range(half * 8, half * 8 + 8):
                used = length_ref[start + p] - gz * tokens
                some = jnp.where(sublane == p % 8, used, some)
                block = held[step, p].astype(jnp.float32)
                block = jnp.where(token < used, block, block[0:1])
                usable[p * tokens : (p + 1) * tokens] = block.astype(jnp.bfloat16)
            any_used = some > 0
            for t in range(ROWS * queries // TILE):
                scores = jnp.dot(
                    usable[half * 8 * tokens : (half + 1) * 8 * tokens],
                    weights[:, t * TILE : (t + 1) * TILE],
                    preferred_element_type=jnp.float32,
                )
                best = []
                for p in range(8):
                    rows = [
                        scores[p * tokens + k : p * tokens + k + 8] for k in range(0, tokens, 8)
                    ]
                    while len(rows) > 1:
                        rows = [jnp.maximum(*rows[k : k + 2]) for k in range(0, len(rows), 2)]
                    best.append(rows[0])
                for level, mask in enumerate(odd):
                    best = [
                        jnp.maximum(
                            jnp.where(mask, b, a),
                            pltpu.roll(jnp.where(mask, a, b), 1 << level, 0),
                        )
                        for a, b in zip(best[::2], best[1::2])
                    ]
                result = jnp.where(any_used, best[0], masked_low)
                for side in range(TILE // queries):
                    parts[step, t * (TILE // queries) + side, half * 8 : half * 8 + 8] = result[
                        :, side * queries : (side + 1) * queries
                    ]

    def one_step(step, carry):
        score(step)

        @pl.when(step == 0)
        def _():
            pl.semaphore_wait(barrier, 21)

        @pl.when(step < SHARE)
        def _():
            relay_copy(step % 2, step // 2, parts.at[step]).start()

        @pl.when(jnp.logical_and(step >= SHARE, step < 3 * SHARE))
        def _():
            near = step - SHARE
            way, joined, turn = near % 2, (near // 2) % 2, near // 4

            @pl.when(joined == 1)
            def _():
                relay_copy(way, turn, parts.at[step]).wait_recv()
                parts[step] = jnp.maximum(parts[step], relay[way, turn])

            final_copy(way, place(step)[1], parts.at[step]).start()

        @pl.when(step >= 3 * SHARE)
        def _():
            piece = place(step)[1]
            for way in range(2):
                final_copy(way, piece, parts.at[step]).wait_recv()
            total = jnp.zeros((CHUNK, queries), jnp.float32)
            for i in range(ROWS):
                best = jnp.maximum(
                    parts[step, i], jnp.maximum(final[0, piece, i], final[1, piece, i])
                )
                total = total + jnp.where(gy * ROWS + i < count_ref[...], best, 0.0)
            sums[gy, piece] = total
            for k in range(1, 4):
                sums_copy(k, piece).start()

        return carry

    lax.fori_loop(0, steps, one_step, 0)

    for piece in range(SHARE):
        for k in range(1, 4):
            sums_copy(k, piece).wait_recv()
    maxsim = (sums[0] + sums[1]) + (sums[2] + sums[3])
    maxsim = maxsim.reshape(SHARE * CHUNK, queries)

    def joined_stats(stats):
        top = jnp.max(stats, axis=0, keepdims=True)
        return top + jnp.log(jnp.sum(jnp.exp(stats - top), axis=0, keepdims=True))

    near_stat[gz] = joined_stats(maxsim)
    for k in range(1, 4):
        near_copy(k).start()
    for k in range(1, 4):
        near_copy(k).wait_recv()
    far_stat[gx] = joined_stats(near_stat[...].reshape(4, queries))
    for k in range(1, 16):
        far_copy(k).start()
    for k in range(1, 16):
        far_copy(k).wait_recv()
    norm = joined_stats(far_stat[...].reshape(16, queries))
    out_ref[...] = (maxsim - norm).T

    for way in range(2):
        for turn in range(2):
            relay_copy(way, turn, parts.at[0]).wait_send()
        for piece in range(SHARE):
            final_copy(way, piece, parts.at[0]).wait_send()
    for k in range(1, 4):
        for piece in range(SHARE):
            sums_copy(k, piece).wait_send()
        near_copy(k).wait_send()
    for k in range(1, 16):
        far_copy(k).wait_send()


def shards(queries, passages, passage_len, query_len):
    count, rows, width = queries.shape
    tokens = passages.shape[1]
    f32 = jnp.float32
    vmem = pl.BlockSpec(memory_space=pltpu.VMEM)
    return pl.pallas_call(
        body,
        out_shape=jax.ShapeDtypeStruct((count, SHARE * CHUNK), f32),
        in_specs=[
            pl.BlockSpec(memory_space=pltpu.SMEM), vmem, vmem, pl.BlockSpec(memory_space=pl.ANY)
        ],
        out_specs=vmem,
        scratch_shapes=[
            pltpu.VMEM((4 * SHARE, CHUNK, tokens, width), jnp.bfloat16),
            pltpu.VMEM((CHUNK * tokens, width), jnp.bfloat16),
            pltpu.VMEM((width, rows * count), jnp.bfloat16),
            pltpu.VMEM((rows * count, width), f32),
            pltpu.VMEM((4 * SHARE, rows, CHUNK, count), f32),
            pltpu.VMEM((2, 2, rows, CHUNK, count), f32),
            pltpu.VMEM((2, SHARE, rows, CHUNK, count), f32),
            pltpu.VMEM((4, SHARE, CHUNK, count), f32),
            pltpu.VMEM((4, 1, count), f32),
            pltpu.VMEM((16, 1, count), f32),
            pltpu.SemaphoreType.DMA((4 * SHARE,)),
            pltpu.SemaphoreType.DMA((2, 2, 2)),
            pltpu.SemaphoreType.DMA((2, 2, SHARE)),
            pltpu.SemaphoreType.DMA((2, 4, SHARE)),
            pltpu.SemaphoreType.DMA((2, 4)),
            pltpu.SemaphoreType.DMA((2, 16)),
        ],
        compiler_params=pltpu.CompilerParams(
            collective_id=0, has_side_effects=True, vmem_limit_bytes=60 * 2**20
        ),
        name="late_interaction",
    )(passage_len, queries, query_len.reshape(1, count), passages)


def solution(mesh):
    return jax.shard_map(
        shards,
        mesh=mesh,
        in_specs=(P(None, "gy", None), P("gx", "gz", None), P("gx"), P()),
        out_specs=P(None, ("gx", "gz")),
        check_vma=False,
    )
```

time: 131 us -> 46.2 us (0.35)
  Pallas kernels: 0 us -> 44.6 us
  matrix products: 38.2 us -> 0 us
  blocking collectives: 32.5 us -> 0 us
  waiting for transfers between devices: 24.4 us -> 0 us
  local copies, waits for them, and re-layouts: 21 us -> 1.47 us
  other arithmetic: 8.28 us -> 0 us
  starting transfers between devices: 4.96 us -> 0 us
    pallas_call x0 -> x1, Pallas kernels: none -> 44.6 us  [shards(): pl.pallas_call(body, out_shape=jax.ShapeDtypeStruct((count, SHARE * CHUNK...]
    dot_general x16 -> x0, matrix products: 38.2 us -> none  [block_maxima(): lax.dot_general(flat_queries, passage_tile, (((1,), (1,)), ((), ())), pre...]
    all_to_all x2 -> x0, blocking collectives: 32.5 us -> none  [copy_for_each(): lax.all_to_all(jnp.broadcast_to(array[None], (devices, *array.shape)), ax...]
    all_to_all x1 -> x0, waiting for transfers between devices: 24.4 us -> none  [shards(): lax.all_to_all(spread, 'gz', split_axis=3, concat_axis=2, tiled=True)]
    another operation x2 -> x0, local copies, waits for them, and re-layouts: 8.32 us -> none  [shards(): spread = maxima.reshape(query_count, query_rows, 1, passage_count)]
    transpose x1 -> x0, local copies, waits for them, and re-layouts: 6.23 us -> none  [token_maxima(): jnp.transpose(pieces, (1, 0, 2))]
    reduce_sum x3 -> x0, other arithmetic: 5.81 us -> none  [the longest x1 5.61 us: shards(): partial_value = jnp.sum(jnp.where(counted, merged, 0.0), axis=1)]
    all_to_all x1 -> x0, starting transfers between devices: 4.96 us -> none  [shards(): lax.all_to_all(spread, 'gz', split_axis=3, concat_axis=2, tiled=True)]
  transfers between devices with their start and end apart: 1 -> 0, of which waited for: 1 -> 0; matrix products, arithmetic and copies ran while one was open for 0% -> 0% of each run, Pallas kernels for 0% -> 0%
where the time goes in v1:
time: 46.2 us; the launch traced here: 46 us
  Pallas kernels  44.6 us (97%)
  local copies, waits for them, and re-layouts  1.47 us (3%)
    pallas_call x1, Pallas kernels, shards(): pl.pallas_call(body, out_shape=jax.ShapeDtypeStruct((count, SHARE * CHUNK...  44.6 us
    unnamed x1, local copies, waits for them, and re-layouts  1.47 us

profile of v1, /device:TPU:1, one launch (start us, length us, event | category | flops | bytes accessed | tf_op | source)
XLA Modules:
  0.0 46.0 jit_solution(10753890177566983767)
XLA Ops:
  0.0 44.6 %late_interaction.1 = f32[128,128]{1,0:T(8,128)} custom-call(s32[512]{0:T(512)} %length_ref.1, bf16[128,8,128]{2,1,0:T(8,128)(2,1)} %query_ref.1, s32[1,128]{1,0:T(1,128)} %bitcast.1, bf16[512,64,128]{2,1,0:T(8,128)(2,1)} %passages_ref.1), custom_call_target="tpu_custom_call" | custom-call | tf_op jit(solution)/shard_map/late_interaction/pallas_call | solution.py:221
  44.6 1.5 %copy.6 = f32[128,128]{1,0:T(8,128)} copy(f32[128,128]{1,0:T(8,128)} %late_interaction.1) | data formatting | bytes 131072

commit v2 on v1

--- a/solution.py
+++ b/solution.py
@@ -1,3 +1,5 @@
+import functools
+
 import jax
 import jax.numpy as jnp
 from jax import lax
@@ -12,6 +14,9 @@
 SHARE = 4
 ROWS = 8
 TILE = 256
+TILES = 3
+FOREIGN = 3
+FIT_THIRD, FIT_LAST = 640, 384
 
 
 def place(step):
@@ -23,7 +28,7 @@
     return offset, jnp.where(is_near, near_piece, far)
 
 
-def body(
+def plain_body(
     length_ref, query_ref, count_ref, passages_ref, out_ref,
     held, usable, weights, wide, parts, relay, final, sums, near_stat, far_stat,
     load_sem, relay_sem, final_sem, sums_sem, near_sem, far_sem,
@@ -213,41 +218,387 @@
         far_copy(k).wait_send()
 
 
-def shards(queries, passages, passage_len, query_len):
-    count, rows, width = queries.shape
-    tokens = passages.shape[1]
-    f32 = jnp.float32
+def packed_body(
+    length_ref, query_ref, count_ref, passages_ref, out_ref,
+    held, raw, choice, owner, weights, wide, given, foreign, far_parts, parts, relay, final,
+    sums, near_stat, far_stat,
+    load_sem, given_sem, relay_sem, final_sem, sums_sem, near_sem, far_sem,
+):
+    gx, gy, gz = lax.axis_index("gx"), lax.axis_index("gy"), lax.axis_index("gz")
+    tokens, width = passages_ref.shape[1:]
+    queries = query_ref.shape[0]
+    f32, bf16 = jnp.float32, jnp.bfloat16
+    half_share = SHARE * CHUNK // 2
+    core = lax.rem(gx, 2)
+    slot = core * 4 + gz
+
+    def start_of(share, piece):
+        offset = jnp.where(share == 0, 2, jnp.where(share == 3, 0, 2 * share - 1))
+        return lax.rem(gz + offset, 4) * (SHARE * CHUNK) + piece * CHUNK
+
+    def load(share, piece):
+        return pltpu.make_async_copy(
+            passages_ref.at[pl.ds(start_of(share, piece), CHUNK)],
+            held.at[share * SHARE + piece], load_sem.at[share * SHARE + piece],
+        )
+
+    def near_place(n):
+        way, joined, turn = n % 2, (n // 2) % 2, n // 4
+        own = n >= 8
+        piece = jnp.where(own, way * 2 + joined, turn + 2 * ((way + joined + 1) % 2))
+        return jnp.where(own, 3, 1 + way), piece
+
+    for piece in range(SHARE):
+        load(jnp.int32(0), piece).start()
+    for n in range(12):
+        load(*near_place(jnp.int32(n))).start()
+
+    def near_peer(k):
+        to_core = lax.rem(core + k // 4, 2)
+        return {"gx": gx - core + to_core, "gz": lax.rem(gz + k % 4, 4)}
+
+    barrier = pltpu.get_barrier_semaphore()
+    peers = [{"gy": lax.rem(gy + k, 4)} for k in range(1, 4)]
+    peers += [near_peer(k) for k in range(1, 8)]
+    peers += [{"gx": lax.rem(gx + 2 * k, 16)} for k in range(1, 8)]
+    foreign[...] = jnp.zeros(foreign.shape, f32)
+    for peer in peers:
+        pl.semaphore_signal(barrier, inc=1, device_id=peer, device_id_type=MESH)
+
+    def given_copy(k, target, to):
+        return pltpu.make_async_remote_copy(
+            src_ref=given.at[k], dst_ref=foreign.at[target],
+            send_sem=given_sem.at[0, k], recv_sem=given_sem.at[1, target],
+            device_id={"gy": to}, device_id_type=MESH,
+        )
+
+    def relay_copy(way, tile):
+        return pltpu.make_async_remote_copy(
+            src_ref=far_parts.at[tile, way], dst_ref=relay.at[way, tile],
+            send_sem=relay_sem.at[0, way, tile], recv_sem=relay_sem.at[1, way, tile],
+            device_id={"gz": lax.rem(gz + 1 + 2 * way, 4)}, device_id_type=MESH,
+        )
+
+    def final_copy(way, piece, source):
+        return pltpu.make_async_remote_copy(
+            src_ref=source, dst_ref=final.at[way, piece],
+            send_sem=final_sem.at[0, way, piece], recv_sem=final_sem.at[1, way, piece],
+            device_id={"gz": lax.rem(gz + 1 + 2 * way, 4)}, device_id_type=MESH,
+        )
+
+    def sums_copy(k, piece):
+        return pltpu.make_async_remote_copy(
+            src_ref=sums.at[gy, piece], dst_ref=sums.at[gy, piece],
+            send_sem=sums_sem.at[0, k, piece], recv_sem=sums_sem.at[1, k, piece],
+            device_id={"gy": lax.rem(gy + k, 4)}, device_id_type=MESH,
+        )
+
+    def near_copy(k):
+        return pltpu.make_async_remote_copy(
+            src_ref=near_stat.at[slot], dst_ref=near_stat.at[slot],
+            send_sem=near_sem.at[0, k], recv_sem=near_sem.at[1, k],
+            device_id=near_peer(k), device_id_type=MESH,
+        )
+
+    def far_copy(k):
+        return pltpu.make_async_remote_copy(
+            src_ref=far_stat.at[gx // 2], dst_ref=far_stat.at[gx // 2],
+            send_sem=far_sem.at[0, k], recv_sem=far_sem.at[1, k],
+            device_id={"gx": lax.rem(gx + 2 * k, 16)}, device_id_type=MESH,
+        )
+
+    wide[...] = query_ref[...].reshape(queries * ROWS, width).astype(f32)
+    given[0] = wide[pl.ds(ROWS - 2, queries, stride=ROWS), :]
+    given[1] = wide[pl.ds(ROWS - 1, queries, stride=ROWS), :]
+
+    @pl.when(gy < 2)
+    def _():
+        pl.semaphore_wait(barrier, 17)
+
+    @pl.when(gy == 0)
+    def _():
+        given_copy(0, 0, 3).start()
+        given_copy(1, 1, 3).start()
+
+    @pl.when(gy == 1)
+    def _():
+        given_copy(1, 2, 3).start()
+        given_copy(0, 0, 2).start()
+
+    for i in range(ROWS):
+        row = wide[pl.ds(i, queries, stride=ROWS), :]
+        raw[:, i * queries : (i + 1) * queries] = row.T.astype(bf16)
+
+    lane = lax.broadcasted_iota(jnp.int32, (queries, 128), 1)
+    line = lax.broadcasted_iota(jnp.int32, (queries, 128), 0)
+    token_of = jnp.where(lane < ROWS, gy * ROWS + lane, 99)
+    token_of = jnp.where(jnp.logical_and(gy < 2, lane >= ROWS - 2), 99, token_of)
+    token_of = jnp.where(jnp.logical_and(gy == 2, lane == ROWS), 14, token_of)
+    for k, token in enumerate((6, 7, 15)):
+        token_of = jnp.where(jnp.logical_and(gy == 3, lane == ROWS + k), token, token_of)
+    lengths = jnp.broadcast_to(count_ref[...].astype(f32), (queries, 128)).T
+    valid = token_of.astype(f32) < lengths
+    one = jnp.where(valid, 1.0, 0.0).astype(bf16)
+    below = jnp.where(lane < line, 1.0, 0.0).astype(bf16)
+    above = jnp.where(line < lane, 1.0, 0.0).astype(bf16)
+    rank = jnp.dot(below, one, preferred_element_type=f32)
+    earlier = jnp.dot(one, above, preferred_element_type=f32).astype(bf16)
+    base = jnp.dot(jnp.ones((queries, 128), bf16), earlier, preferred_element_type=f32)
+    gap = jnp.maximum(TILE - base[:, ROWS : ROWS + 1], 0.0)
+    place_of = rank + base + jnp.where(lane >= ROWS, gap, 0.0)
+    place_of = jnp.where(valid, place_of, -1.0)
+    lane_wide = lax.broadcasted_iota(jnp.int32, (queries, TILE), 1).astype(f32)
+
+    def pack(tile):
+        slots = ROWS if tile == 0 else ROWS + FOREIGN
+        taken = jnp.zeros((queries, TILE), f32)
+        for s in range(slots):
+            hit = jnp.where(place_of[:, s : s + 1] == lane_wide + float(tile * TILE), 1.0, 0.0)
+            taken = taken + hit
+            choice[s * queries : (s + 1) * queries] = hit.astype(bf16)
+        owner[tile] = taken.astype(bf16)
+        weights[tile] = jnp.dot(
+            raw[:, : slots * queries], choice[: slots * queries], preferred_element_type=f32
+        ).astype(bf16)
+
+    sublane = lax.broadcasted_iota(jnp.int32, (8, TILE), 0)
+    odd = [(sublane & k) != 0 for k in (1, 2, 4)]
+    token = lax.broadcasted_iota(jnp.int32, (tokens, width), 0)
+
+    def score(index, start, fix, tiles, put):
+        for eighth in range(CHUNK // 8):
+            some = jnp.zeros((8, TILE), jnp.int32)
+            for p in range(eighth * 8, eighth * 8 + 8):
+                used = length_ref[start + p] - gz * tokens
+                some = jnp.where(sublane == p % 8, used, some)
+                if fix:
+                    block = held[index, p].astype(f32)
+                    held[index, p] = jnp.where(token < used, block, block[0:1]).astype(bf16)
+            any_used = some > 0
+            block = held[index, eighth * 8 : eighth * 8 + 8].reshape(8 * tokens, width)
+            for t in tiles:
+                scores = jnp.dot(block, weights[t], preferred_element_type=f32)
+                best = []
+                for p in range(8):
+                    rows = [
+                        scores[p * tokens + k : p * tokens + k + 8] for k in range(0, tokens, 8)
+                    ]
+                    while len(rows) > 1:
+                        rows = [jnp.maximum(*rows[k : k + 2]) for k in range(0, len(rows), 2)]
+                    best.append(rows[0])
+                for level, mask in enumerate(odd):
+                    best = [
+                        jnp.maximum(
+                            jnp.where(mask, b, a),
+                            pltpu.roll(jnp.where(mask, a, b), 1 << level, 0),
+                        )
+                        for a, b in zip(best[::2], best[1::2])
+                    ]
+                put(t, eighth * 8, jnp.where(any_used, best[0], masked_low))
+
+    for tile in range(TILES):
+        if tile == 1:
+
+            @pl.when(gy == 2)
+            def _():
+                given_copy(0, 0, 2).wait_recv()
+
+            @pl.when(gy == 3)
+            def _():
+                for k in range(FOREIGN):
+                    given_copy(0, k, 3).wait_recv()
+
+            for k in range(FOREIGN):
+                raw[:, (ROWS + k) * queries : (ROWS + k + 1) * queries] = foreign[k].T.astype(bf16)
+        pack(tile)
+        for piece in range(SHARE):
+            if tile == 0:
+                load(jnp.int32(0), piece).wait()
+
+            def put(t, row, value, piece=piece):
+                row = piece % 2 * CHUNK + row
+                far_parts[t, piece // 2, row : row + 8] = value
+
+            score(piece, start_of(jnp.int32(0), piece), tile == 0, (tile,), put)
+        if tile == 0:
+
+            @pl.when(gy >= 2)
+            def _():
+                pl.semaphore_wait(barrier, 17)
+
+        for way in range(2):
+            relay_copy(way, tile).start()
+
+    def later(n, carry):
+        share, piece = near_place(n)
+        load(share, piece).wait()
+
+        def put(t, row, value):
+            parts[n, t, row : row + 8] = value
+
+        score(share * SHARE + piece, start_of(share, piece), True, range(TILES), put)
+
+        @pl.when(n < 8)
+        def _():
+            way, joined, turn = n % 2, (n // 2) % 2, n // 4
+
+            @pl.when(jnp.logical_and(joined == 1, turn == 0))
+            def _():
+                for tile in range(TILES):
+                    relay_copy(way, tile).wait_recv()
+
+            @pl.when(joined == 1)
+            def _():
+                for tile in range(TILES):
+                    parts[n, tile] = jnp.maximum(
+                        parts[n, tile], relay[way, tile, pl.ds(turn * CHUNK, CHUNK)]
+                    )
+
+            final_copy(way, piece, parts.at[n]).start()
+
+        @pl.when(n >= 8)
+        def _():
+            for way in range(2):
+                final_copy(way, piece, parts.at[n]).wait_recv()
+            total = jnp.zeros((CHUNK, queries), f32)
+            for tile in range(TILES):
+                best = jnp.maximum(
+                    parts[n, tile], jnp.maximum(final[0, piece, tile], final[1, piece, tile])
+                )
+                for _ in range(3):
+                    term = best.astype(bf16)
+                    total = total + lax.dot_general(
+                        term, owner[tile], (((1,), (1,)), ((), ())), preferred_element_type=f32
+                    )
+                    best = best - term.astype(f32)
+            sums[gy, piece] = total
+            for k in range(1, 4):
+                sums_copy(k, piece).start()
+
+        return carry
+
+    lax.fori_loop(0, 12, later, 0)
+
+    for piece in range(SHARE):
+        for k in range(1, 4):
+            sums_copy(k, piece).wait_recv()
+    maxsim = (sums[0] + sums[1]) + (sums[2] + sums[3])
+    maxsim = maxsim.reshape(SHARE * CHUNK, queries)
+
+    def joined_stats(stats):
+        top = jnp.max(stats, axis=0, keepdims=True)
+        return top + jnp.log(jnp.sum(jnp.exp(stats - top), axis=0, keepdims=True))
+
+    near_stat[slot] = joined_stats(maxsim)
+    for k in range(1, 8):
+        near_copy(k).start()
+    for k in range(1, 8):
+        near_copy(k).wait_recv()
+    far_stat[gx // 2] = joined_stats(near_stat[...].reshape(8, queries))
+    for k in range(1, 8):
+        far_copy(k).start()
+    for k in range(1, 8):
+        far_copy(k).wait_recv()
+    norm = joined_stats(far_stat[...].reshape(8, queries))
+    out_ref[...] = (maxsim - norm).T
+
+    @pl.when(gy < 2)
+    def _():
+        for k in range(2):
+            given_copy(k, 0, 3).wait_send()
+
+    for way in range(2):
+        for tile in range(TILES):
+            relay_copy(way, tile).wait_send()
+        for piece in range(SHARE):
+            final_copy(way, piece, parts.at[0]).wait_send()
+    for k in range(1, 4):
+        for piece in range(SHARE):
+            sums_copy(k, piece).wait_send()
+    for k in range(1, 8):
+        near_copy(k).wait_send()
+        far_copy(k).wait_send()
+
+
+def call(body, name, collective, scratch, lengths, queries, counts, passages):
     vmem = pl.BlockSpec(memory_space=pltpu.VMEM)
     return pl.pallas_call(
         body,
-        out_shape=jax.ShapeDtypeStruct((count, SHARE * CHUNK), f32),
+        out_shape=jax.ShapeDtypeStruct((queries.shape[0], SHARE * CHUNK), jnp.float32),
         in_specs=[
             pl.BlockSpec(memory_space=pltpu.SMEM), vmem, vmem, pl.BlockSpec(memory_space=pl.ANY)
         ],
         out_specs=vmem,
-        scratch_shapes=[
-            pltpu.VMEM((4 * SHARE, CHUNK, tokens, width), jnp.bfloat16),
-            pltpu.VMEM((CHUNK * tokens, width), jnp.bfloat16),
-            pltpu.VMEM((width, rows * count), jnp.bfloat16),
-            pltpu.VMEM((rows * count, width), f32),
-            pltpu.VMEM((4 * SHARE, rows, CHUNK, count), f32),
-            pltpu.VMEM((2, 2, rows, CHUNK, count), f32),
-            pltpu.VMEM((2, SHARE, rows, CHUNK, count), f32),
-            pltpu.VMEM((4, SHARE, CHUNK, count), f32),
-            pltpu.VMEM((4, 1, count), f32),
-            pltpu.VMEM((16, 1, count), f32),
-            pltpu.SemaphoreType.DMA((4 * SHARE,)),
-            pltpu.SemaphoreType.DMA((2, 2, 2)),
-            pltpu.SemaphoreType.DMA((2, 2, SHARE)),
-            pltpu.SemaphoreType.DMA((2, 4, SHARE)),
-            pltpu.SemaphoreType.DMA((2, 4)),
-            pltpu.SemaphoreType.DMA((2, 16)),
-        ],
+        scratch_shapes=scratch,
         compiler_params=pltpu.CompilerParams(
-            collective_id=0, has_side_effects=True, vmem_limit_bytes=60 * 2**20
+            collective_id=collective, has_side_effects=True, vmem_limit_bytes=60 * 2**20
         ),
-        name="late_interaction",
-    )(passage_len, queries, query_len.reshape(1, count), passages)
+        name=name,
+    )(lengths, queries, counts, passages)
+
+
+def shards(queries, passages, passage_len, query_len):
+    count, rows, width = queries.shape
+    tokens = passages.shape[1]
+    f32, bf16 = jnp.float32, jnp.bfloat16
+    dma = pltpu.SemaphoreType.DMA
+    plain = [
+        pltpu.VMEM((4 * SHARE, CHUNK, tokens, width), bf16),
+        pltpu.VMEM((CHUNK * tokens, width), bf16),
+        pltpu.VMEM((width, rows * count), bf16),
+        pltpu.VMEM((rows * count, width), f32),
+        pltpu.VMEM((4 * SHARE, rows, CHUNK, count), f32),
+        pltpu.VMEM((2, 2, rows, CHUNK, count), f32),
+        pltpu.VMEM((2, SHARE, rows, CHUNK, count), f32),
+        pltpu.VMEM((4, SHARE, CHUNK, count), f32),
+        pltpu.VMEM((4, 1, count), f32),
+        pltpu.VMEM((16, 1, count), f32),
+        dma((4 * SHARE,)),
+        dma((2, 2, 2)),
+        dma((2, 2, SHARE)),
+        dma((2, 4, SHARE)),
+        dma((2, 4)),
+        dma((2, 16)),
+    ]
+    packed = [
+        pltpu.VMEM((4 * SHARE, CHUNK, tokens, width), bf16),
+        pltpu.VMEM((width, (rows + FOREIGN) * count), bf16),
+        pltpu.VMEM(((rows + FOREIGN) * count, TILE), bf16),
+        pltpu.VMEM((TILES, count, TILE), bf16),
+        pltpu.VMEM((TILES, width, TILE), bf16),
+        pltpu.VMEM((rows * count, width), f32),
+        pltpu.VMEM((2, count, width), f32),
+        pltpu.VMEM((FOREIGN, count, width), f32),
+        pltpu.VMEM((TILES, 2, SHARE * CHUNK // 2, TILE), f32),
+        pltpu.VMEM((12, TILES, CHUNK, TILE), f32),
+        pltpu.VMEM((2, TILES, SHARE * CHUNK // 2, TILE), f32),
+        pltpu.VMEM((2, SHARE, TILES, CHUNK, TILE), f32),
+        pltpu.VMEM((4, SHARE, CHUNK, count), f32),
+        pltpu.VMEM((8, 1, count), f32),
+        pltpu.VMEM((8, 1, count), f32),
+        dma((4 * SHARE,)),
+        dma((2, FOREIGN)),
+        dma((2, 2, TILES)),
+        dma((2, 2, SHARE)),
+        dma((2, 4, SHARE)),
+        dma((2, 8)),
+        dma((2, 8)),
+    ]
+    third = jnp.clip(query_len - 2 * rows, 0, rows)
+    last = jnp.clip(query_len - 3 * rows, 0, rows)
+    counted = jnp.sum(third + last * 4096)
+    fits = jnp.logical_and(
+        (counted & 4095) <= FIT_THIRD, lax.shift_right_logical(counted, 12) <= FIT_LAST
+    )
+    return lax.cond(
+        fits,
+        functools.partial(call, packed_body, "packed_scores", 0, packed),
+        functools.partial(call, plain_body, "plain_scores", 1, plain),
+        passage_len,
+        queries,
+        query_len.reshape(1, count),
+        passages,
+    )
 
 
 def solution(mesh):

time: 46.2 us -> 49.5 us (1.071)
  Pallas kernels: 44.6 us -> 46.1 us
  other arithmetic: 0 us -> 1.3 us
  between operations: 0.01 us -> 1.31 us
  local copies, waits for them, and re-layouts: 1.47 us -> 0.63 us
    pallas_call x1, Pallas kernels: 44.6 us -> 46.1 us  [call(): pl.pallas_call(body, out_shape=jax.ShapeDtypeStruct((queries.shape[0], SH...]
    reduce_sum x0 -> x1, other arithmetic: none -> 1.3 us  [shards(): counted = jnp.sum(third + last * 4096)]
    unnamed x1, local copies, waits for them, and re-layouts: 1.47 us -> 0.63 us
where the time goes in v2:
time: 49.5 us; the launch traced here: 49.4 us
  Pallas kernels  46.1 us (93%)
  between operations  1.31 us (3%)
  other arithmetic  1.3 us (3%)
  local copies, waits for them, and re-layouts  0.63 us (1%)
    pallas_call x1, Pallas kernels, call(): pl.pallas_call(body, out_shape=jax.ShapeDtypeStruct((queries.shape[0], SH...  46.1 us
    reduce_sum x1, other arithmetic, shards(): counted = jnp.sum(third + last * 4096)  1.3 us

profile of v2, /device:TPU:1, one launch (start us, length us, event | category | flops | bytes accessed | tf_op | source)
XLA Modules:
  0.0 49.4 jit_solution(16821705316777169960)
XLA Ops:
  0.0 1.3 %add_reduce_fusion = s32[]{:T(128)} fusion(s32[128]{0:T(128)} %param.9), kind=kLoop, calls=%fused_computation | loop fusion | flops 895 | bytes 516 | tf_op jit(solution)/shard_map/reduce_sum | solution.py:589
  2.6 46.1 %conditional.1 = (f32[128,128]{1,0:T(8,128)S(1)}) conditional(s32[]{:T(128)} %convert_element_type.3, (s32[512]{0:T(512)}, bf16[128,8,128]{2,1,0:T(8,128)(2,1)}, s32[128]{0:T(128)}, bf16[512,64,128]{2,1,0:T(8,128)(2,1)}) %tuple.11, (s32[512]{0:T(512)}, bf16[128,8,128]{2,1,0:T(8,128)(2,1)}, s32[128]{0:T(128)}, bf16[512,64,128]{2,1,0:T(8,128)(2,1)}) %tuple.11), branch_computations={%region_1.2_spmd, %region_2.3_spmd} | conditional | bytes 8 | solution.py:593
  2.6 46.1 %packed_scores.1 = f32[128,128]{1,0:T(8,128)S(1)} custom-call(s32[512]{0:T(512)} %get-tuple-element.42.length_ref, bf16[128,8,128]{2,1,0:T(8,128)(2,1)} %get-tuple-element.44.query_ref, s32[1,128]{1,0:T(1,128)} %bitcast.3, bf16[512,64,128]{2,1,0:T(8,128)(2,1)} %get-tuple-element.46.passages_ref), custom_call_target="tpu_custom_call" | custom-call | tf_op jit(solution)/shard_map/cond/branch_1_fun/packed_scores/pallas_call | solution.py:525
  48.7 0.6 %copy.16 = f32[128,128]{1,0:T(8,128)} copy(f32[128,128]{1,0:T(8,128)S(1)} %get-tuple-element.32) | data formatting | bytes 131072

commit v3 on v1

v3 whole, which is shorter than its diff:
```python
import jax
import jax.numpy as jnp
from jax import lax
from jax.experimental import pallas as pl
from jax.experimental.pallas import tpu as pltpu
from jax.sharding import PartitionSpec as P

masked_low = -1e30
MESH = pl.DeviceIdType.MESH

PIECE = 32
SHARE = 4
HALF = PIECE * SHARE // 2
ROWS = 8
TILE = 256
FAR = ((0, 16), (16, 16), (32, 32))


def body(
    length_ref, query_ref, count_ref, passages_ref, out_ref,
    held, usable, weights, wide, far_parts, near_parts, own_parts, relay, final, sums,
    near_stat, far_stat,
    load_sem, relay_sem, final_sem, sums_sem, near_sem, far_sem,
):
    gx, gy, gz = lax.axis_index("gx"), lax.axis_index("gy"), lax.axis_index("gz")
    tokens, width = passages_ref.shape[1:]
    queries = query_ref.shape[0]
    share_rows = SHARE * PIECE
    core = lax.rem(gx, 2)
    slot = core * 4 + gz

    def start_of(share):
        offset = jnp.where(share == 2, 2, jnp.where(share == 3, 0, 1 + 2 * share))
        return lax.rem(gz + offset, 4) * share_rows

    def load(share, row, count, sem):
        return pltpu.make_async_copy(
            passages_ref.at[pl.ds(start_of(share) + row, count)],
            held.at[pl.ds(share * share_rows + row, count)], load_sem.at[sem],
        )

    def near_piece(way, n):
        joined, turn = n // 2, n % 2
        return turn + 2 * ((way + joined + 1) % 2)

    def far_load(way, k):
        return load(2, way * HALF + FAR[k][0], FAR[k][1], way * 3 + k)

    def near_load(way, n):
        return load(way, near_piece(way, n) * PIECE, PIECE, 6 + way * SHARE + n)

    def own_load(n):
        return load(3, own_piece(n) * PIECE, PIECE, 14 + n)

    def own_piece(n):
        return (n % 2) * 2 + n // 2

    for k in range(len(FAR)):
        for way in range(2):
            far_load(way, k).start()
    for n in range(SHARE):
        for way in range(2):
            near_load(way, n).start()
    for n in range(SHARE):
        own_load(n).start()

    def near_peer(k):
        to_core = lax.rem(core + k // 4, 2)
        return {"gx": gx - core + to_core, "gz": lax.rem(gz + k % 4, 4)}

    barrier = pltpu.get_barrier_semaphore()
    peers = [{"gy": lax.rem(gy + k, 4)} for k in range(1, 4)]
    peers += [near_peer(k) for k in range(1, 8)]
    peers += [{"gx": lax.rem(gx + 2 * k, 16)} for k in range(1, 8)]
    for peer in peers:
        pl.semaphore_signal(barrier, inc=1, device_id=peer, device_id_type=MESH)

    wide[...] = query_ref[...].reshape(queries * ROWS, width).astype(jnp.float32)
    for i in range(ROWS):
        row = wide[pl.ds(i, queries, stride=ROWS), :]
        weights[:, i * queries : (i + 1) * queries] = row.T.astype(jnp.bfloat16)

    sublane = lax.broadcasted_iota(jnp.int32, (8, TILE), 0)
    odd = [(sublane & k) != 0 for k in (1, 2, 4)]
    token = lax.broadcasted_iota(jnp.int32, (tokens, width), 0)

    def relay_copy(way, k):
        rows = pl.ds(*FAR[k])
        return pltpu.make_async_remote_copy(
            src_ref=far_parts.at[way, rows], dst_ref=relay.at[way, rows],
            send_sem=relay_sem.at[0, way, k], recv_sem=relay_sem.at[1, way, k],
            device_id={"gz": lax.rem(gz + 1 + 2 * way, 4)}, device_id_type=MESH,
        )

    def final_copy(way, piece, source):
        return pltpu.make_async_remote_copy(
            src_ref=source, dst_ref=final.at[way, piece],
            send_sem=final_sem.at[0, way, piece], recv_sem=final_sem.at[1, way, piece],
            device_id={"gz": lax.rem(gz + 1 + 2 * way, 4)}, device_id_type=MESH,
        )

    def sums_copy(k, piece):
        return pltpu.make_async_remote_copy(
            src_ref=sums.at[gy, piece], dst_ref=sums.at[gy, piece],
            send_sem=sums_sem.at[0, k, piece], recv_sem=sums_sem.at[1, k, piece],
            device_id={"gy": lax.rem(gy + k, 4)}, device_id_type=MESH,
        )

    def near_copy(k):
        return pltpu.make_async_remote_copy(
            src_ref=near_stat.at[slot], dst_ref=near_stat.at[slot],
            send_sem=near_sem.at[0, k], recv_sem=near_sem.at[1, k],
            device_id=near_peer(k), device_id_type=MESH,
        )

    def far_copy(k):
        return pltpu.make_async_remote_copy(
            src_ref=far_stat.at[gx // 2], dst_ref=far_stat.at[gx // 2],
            send_sem=far_sem.at[0, k], recv_sem=far_sem.at[1, k],
            device_id={"gx": lax.rem(gx + 2 * k, 16)}, device_id_type=MESH,
        )

    def score(share, row, count, put):
        first = share * share_rows + row
        for group in range(count // 8):
            some = jnp.zeros((8, TILE), jnp.int32)
            for p in range(8):
                at = group * 8 + p
                used = length_ref[start_of(share) + row + at] - gz * tokens
                some = jnp.where(sublane == p, used, some)
                block = held[first + at].astype(jnp.float32)
                block = jnp.where(token < used, block, block[0:1])
                usable[at * tokens : (at + 1) * tokens] = block.astype(jnp.bfloat16)
            any_used = some > 0
            for t in range(ROWS * queries // TILE):
                scores = jnp.dot(
                    usable[group * 8 * tokens : (group + 1) * 8 * tokens],
                    weights[:, t * TILE : (t + 1) * TILE],
                    preferred_element_type=jnp.float32,
                )
                best = []
                for p in range(8):
                    rows = [
                        scores[p * tokens + k : p * tokens + k + 8] for k in range(0, tokens, 8)
                    ]
                    while len(rows) > 1:
                        rows = [jnp.maximum(*rows[k : k + 2]) for k in range(0, len(rows), 2)]
                    best.append(rows[0])
                for level, mask in enumerate(odd):
                    best = [
                        jnp.maximum(
                            jnp.where(mask, b, a),
                            pltpu.roll(jnp.where(mask, a, b), 1 << level, 0),
                        )
                        for a, b in zip(best[::2], best[1::2])
                    ]
                put(group * 8, t, jnp.where(any_used, best[0], masked_low))

    def into(*at):
        def put(row, t, value):
            at[0][(*at[1:-1], pl.ds(at[-1] + row, 8), pl.ds(t * TILE, TILE))] = value

        return put

    for k, (row, count) in enumerate(FAR):
        for way in range(2):
            far_load(way, k).wait()
        for way in range(2):
            score(2, way * HALF + row, count, into(far_parts, way, row))
        if k == 0:
            pl.semaphore_wait(barrier, 17)
        for way in range(2):
            relay_copy(way, k).start()

    def near_step(n, carry):
        for way in range(2):
            near_load(way, n).wait()
        for way in range(2):
            score(way, near_piece(way, n) * PIECE, PIECE, into(near_parts, n, way, 0))

        @pl.when(n == 2)
        def _():
            for way in range(2):
                for k in range(len(FAR)):
                    relay_copy(way, k).wait_recv()

        @pl.when(n >= 2)
        def _():
            rows = pl.ds((n - 2) * PIECE, PIECE)
            for way in range(2):
                near_parts[n, way] = jnp.maximum(near_parts[n, way], relay[way, rows])

        for way in range(2):
            final_copy(way, near_piece(way, n), near_parts.at[n, way]).start()
        return carry

    lax.fori_loop(0, SHARE, near_step, 0)

    def own_step(m, carry):
        for side in range(2):
            own_load(2 * m + side).wait()
        for side in range(2):
            n = 2 * m + side
            score(3, own_piece(n) * PIECE, PIECE, into(own_parts, n, 0))
        return carry

    lax.fori_loop(0, SHARE // 2, own_step, 0)

    def finish(n, carry):
        piece = own_piece(n)
        for way in range(2):
            final_copy(way, piece, own_parts.at[n]).wait_recv()
        total = jnp.zeros((PIECE, queries), jnp.float32)
        for i in range(ROWS):
            lanes = slice(i * queries, (i + 1) * queries)
            best = jnp.maximum(
                own_parts[n, :, lanes],
                jnp.maximum(final[0, piece, :, lanes], final[1, piece, :, lanes]),
            )
            total = total + jnp.where(gy * ROWS + i < count_ref[...], best, 0.0)
        sums[gy, piece] = total
        for k in (2, 1, 3):
            sums_copy(k, piece).start()
        return carry

    lax.fori_loop(0, SHARE, finish, 0)

    for piece in range(SHARE):
        for k in range(1, 4):
            sums_copy(k, piece).wait_recv()
    maxsim = (sums[0] + sums[1]) + (sums[2] + sums[3])
    maxsim = maxsim.reshape(share_rows, queries)

    def joined_stats(stats):
        top = jnp.max(stats, axis=0, keepdims=True)
        return top + jnp.log(jnp.sum(jnp.exp(stats - top), axis=0, keepdims=True))

    near_stat[slot] = joined_stats(maxsim)
    for k in (6, 2, 5, 7, 1, 3, 4):
        near_copy(k).start()
    for k in range(1, 8):
        near_copy(k).wait_recv()
    far_stat[gx // 2] = joined_stats(near_stat[...].reshape(8, queries))
    for k in (4, 3, 5, 2, 6, 1, 7):
        far_copy(k).start()
    for k in range(1, 8):
        far_copy(k).wait_recv()
    norm = joined_stats(far_stat[...].reshape(8, queries))
    out_ref[...] = (maxsim - norm).T

    for way in range(2):
        for k in range(len(FAR)):
            relay_copy(way, k).wait_send()
        for piece in range(SHARE):
            final_copy(way, piece, own_parts.at[0]).wait_send()
    for k in range(1, 4):
        for piece in range(SHARE):
            sums_copy(k, piece).wait_send()
    for k in range(1, 8):
        near_copy(k).wait_send()
        far_copy(k).wait_send()


def shards(queries, passages, passage_len, query_len):
    count, rows, width = queries.shape
    tokens = passages.shape[1]
    f32 = jnp.float32
    vmem = pl.BlockSpec(memory_space=pltpu.VMEM)
    dma = pltpu.SemaphoreType.DMA
    lanes = rows * count
    return pl.pallas_call(
        body,
        out_shape=pltpu.VMEM((count, SHARE * PIECE), f32),
        in_specs=[
            pl.BlockSpec(memory_space=pltpu.SMEM), vmem, vmem, pl.BlockSpec(memory_space=pl.ANY)
        ],
        out_specs=vmem,
        scratch_shapes=[
            pltpu.VMEM(passages.shape, passages.dtype),
            pltpu.VMEM((2 * PIECE * tokens, width), jnp.bfloat16),
            pltpu.VMEM((width, lanes), jnp.bfloat16),
            pltpu.VMEM((lanes, width), f32),
            pltpu.VMEM((2, HALF, lanes), f32),
            pltpu.VMEM((SHARE, 2, PIECE, lanes), f32),
            pltpu.VMEM((SHARE, PIECE, lanes), f32),
            pltpu.VMEM((2, HALF, lanes), f32),
            pltpu.VMEM((2, SHARE, PIECE, lanes), f32),
            pltpu.VMEM((4, SHARE, PIECE, count), f32),
            pltpu.VMEM((8, 1, count), f32),
            pltpu.VMEM((8, 1, count), f32),
            dma((6 + 3 * SHARE,)),
            dma((2, 2, len(FAR))),
            dma((2, 2, SHARE)),
            dma((2, 4, SHARE)),
            dma((2, 8)),
            dma((2, 8)),
        ],
        compiler_params=pltpu.CompilerParams(
            collective_id=0, has_side_effects=True, vmem_limit_bytes=60 * 2**20
        ),
        name="late_interaction",
    )(passage_len, queries, query_len.reshape(1, count), passages)


def solution(mesh):
    return jax.shard_map(
        shards,
        mesh=mesh,
        in_specs=(P(None, "gy", None), P("gx", "gz", None), P("gx"), P()),
        out_specs=P(None, ("gx", "gz")),
        check_vma=False,
    )
```

time: 46.2 us -> 43.2 us (0.935)
  Pallas kernels: 44.6 us -> 42.5 us
  local copies, waits for them, and re-layouts: 1.47 us -> 0.63 us
    pallas_call x1, Pallas kernels: 44.6 us -> 42.5 us  [shards(): pl.pallas_call(body, out_shape=pltpu.VMEM((count, SHARE * PIECE), f32), i...]
    unnamed x1, local copies, waits for them, and re-layouts: 1.47 us -> 0.63 us
where the time goes in v3:
time: 43.2 us; the launch traced here: 43.1 us
  Pallas kernels  42.5 us (98%)
  local copies, waits for them, and re-layouts  0.63 us (1%)
    pallas_call x1, Pallas kernels, shards(): pl.pallas_call(body, out_shape=pltpu.VMEM((count, SHARE * PIECE), f32), i...  42.5 us

profile of v3, /device:TPU:1, one launch (start us, length us, event | category | flops | bytes accessed | tf_op | source)
XLA Modules:
  0.0 43.1 jit_solution(16119285254669930010)
XLA Ops:
  0.0 42.5 %late_interaction.1 = f32[128,128]{1,0:T(8,128)S(1)} custom-call(s32[512]{0:T(512)} %length_ref.1, bf16[128,8,128]{2,1,0:T(8,128)(2,1)} %query_ref.1, s32[1,128]{1,0:T(1,128)} %bitcast.1, bf16[512,64,128]{2,1,0:T(8,128)(2,1)} %passages_ref.1), custom_call_target="tpu_custom_call" | custom-call | tf_op jit(solution)/shard_map/late_interaction/pallas_call | solution.py:271
  42.5 0.6 %copy.6 = f32[128,128]{1,0:T(8,128)} copy(f32[128,128]{1,0:T(8,128)S(1)} %late_interaction.1) | data formatting | bytes 131072

commit v4 on v3

--- a/solution.py
+++ b/solution.py
@@ -18,7 +18,7 @@
 
 def body(
     length_ref, query_ref, count_ref, passages_ref, out_ref,
-    held, usable, weights, wide, far_parts, near_parts, own_parts, relay, final, sums,
+    held, used_ref, usable, weights, wide, far_parts, near_parts, own_parts, relay, final, sums,
     near_stat, far_stat,
     load_sem, relay_sem, final_sem, sums_sem, near_sem, far_sem,
 ):
@@ -80,6 +80,11 @@
         row = wide[pl.ds(i, queries, stride=ROWS), :]
         weights[:, i * queries : (i + 1) * queries] = row.T.astype(jnp.bfloat16)
 
+    for k in range(passages_ref.shape[0] // 128):
+        row = length_ref[:, k * 128 : (k + 1) * 128].astype(jnp.float32)
+        row = jnp.broadcast_to(row, (128, 128)).T.astype(jnp.int32)
+        used_ref[k * 128 : (k + 1) * 128] = row - gz * tokens
+
     sublane = lax.broadcasted_iota(jnp.int32, (8, TILE), 0)
     odd = [(sublane & k) != 0 for k in (1, 2, 4)]
     token = lax.broadcasted_iota(jnp.int32, (tokens, width), 0)
@@ -123,15 +128,14 @@
     def score(share, row, count, put):
         first = share * share_rows + row
         for group in range(count // 8):
-            some = jnp.zeros((8, TILE), jnp.int32)
+            used = used_ref[pl.ds(pl.multiple_of(start_of(share) + row + group * 8, 8), 8), :]
             for p in range(8):
                 at = group * 8 + p
-                used = length_ref[start_of(share) + row + at] - gz * tokens
-                some = jnp.where(sublane == p, used, some)
-                block = held[first + at].astype(jnp.float32)
-                block = jnp.where(token < used, block, block[0:1])
-                usable[at * tokens : (at + 1) * tokens] = block.astype(jnp.bfloat16)
-            any_used = some > 0
+                block = held[first + at]
+                usable[at * tokens : (at + 1) * tokens] = jnp.where(
+                    token < used[p : p + 1], block, block[0:1]
+                )
+            any_used = jnp.concatenate([used, used], axis=1) > 0
             for t in range(ROWS * queries // TILE):
                 scores = jnp.dot(
                     usable[group * 8 * tokens : (group + 1) * 8 * tokens],
@@ -272,11 +276,12 @@
         body,
         out_shape=pltpu.VMEM((count, SHARE * PIECE), f32),
         in_specs=[
-            pl.BlockSpec(memory_space=pltpu.SMEM), vmem, vmem, pl.BlockSpec(memory_space=pl.ANY)
+            vmem, vmem, vmem, pl.BlockSpec(memory_space=pl.ANY)
         ],
         out_specs=vmem,
         scratch_shapes=[
             pltpu.VMEM(passages.shape, passages.dtype),
+            pltpu.VMEM((passages.shape[0], 128), jnp.int32),
             pltpu.VMEM((2 * PIECE * tokens, width), jnp.bfloat16),
             pltpu.VMEM((width, lanes), jnp.bfloat16),
             pltpu.VMEM((lanes, width), f32),
@@ -299,7 +304,7 @@
             collective_id=0, has_side_effects=True, vmem_limit_bytes=60 * 2**20
         ),
         name="late_interaction",
-    )(passage_len, queries, query_len.reshape(1, count), passages)
+    )(passage_len.reshape(1, -1), queries, query_len.reshape(1, count), passages)
 
 
 def solution(mesh):

time: 43.2 us -> 43.2 us (level)
  no operation moved by 1% of the time
where the time goes in v4:
time: 43.2 us; the launch traced here: 43.1 us
  Pallas kernels  42.5 us (98%)
  local copies, waits for them, and re-layouts  0.63 us (1%)
    pallas_call x1, Pallas kernels, shards(): pl.pallas_call(body, out_shape=pltpu.VMEM((count, SHARE * PIECE), f32), i...  42.5 us

profile of v4, /device:TPU:1, one launch (start us, length us, event | category | flops | bytes accessed | tf_op | source)
XLA Modules:
  0.0 43.1 jit_solution(4665297803549264875)
XLA Ops:
  0.0 42.5 %late_interaction.1 = f32[128,128]{1,0:T(8,128)S(1)} custom-call(s32[1,512]{1,0:T(1,128)} %bitcast.2, bf16[128,8,128]{2,1,0:T(8,128)(2,1)} %query_ref.1, s32[1,128]{1,0:T(1,128)} %bitcast.3, bf16[512,64,128]{2,1,0:T(8,128)(2,1)} %passages_ref.1), custom_call_target="tpu_custom_call" | custom-call | tf_op jit(solution)/shard_map/late_interaction/pallas_call | solution.py:275
  42.5 0.6 %copy.6 = f32[128,128]{1,0:T(8,128)} copy(f32[128,128]{1,0:T(8,128)S(1)} %late_interaction.1) | data formatting | bytes 131072

commit v5 on v4

--- a/solution.py
+++ b/solution.py
@@ -80,11 +80,13 @@
         row = wide[pl.ds(i, queries, stride=ROWS), :]
         weights[:, i * queries : (i + 1) * queries] = row.T.astype(jnp.bfloat16)
 
-    for k in range(passages_ref.shape[0] // 128):
-        row = length_ref[:, k * 128 : (k + 1) * 128].astype(jnp.float32)
-        row = jnp.broadcast_to(row, (128, 128)).T.astype(jnp.int32)
-        used_ref[k * 128 : (k + 1) * 128] = row - gz * tokens
-
+    def lay_out(share):
+        rows = pl.ds(pl.multiple_of(start_of(share), share_rows), share_rows)
+        row = length_ref[:, rows].astype(jnp.float32)
+        row = jnp.broadcast_to(row, (share_rows, 128)).T.astype(jnp.int32)
+        used_ref[rows] = row - gz * tokens
+
+    lay_out(2)
     sublane = lax.broadcasted_iota(jnp.int32, (8, TILE), 0)
     odd = [(sublane & k) != 0 for k in (1, 2, 4)]
     token = lax.broadcasted_iota(jnp.int32, (tokens, width), 0)
@@ -175,6 +177,9 @@
             pl.semaphore_wait(barrier, 17)
         for way in range(2):
             relay_copy(way, k).start()
+        if k == 0:
+            for share in (0, 1, 3):
+                lay_out(share)
 
     def near_step(n, carry):
         for way in range(2):

time: 43.2 us -> 43.3 us (level)
  no operation moved by 1% of the time
where the time goes in v5:
time: 43.3 us; the launch traced here: 43.2 us
  Pallas kernels  42.6 us (98%)
  local copies, waits for them, and re-layouts  0.63 us (1%)
    pallas_call x1, Pallas kernels, shards(): pl.pallas_call(body, out_shape=pltpu.VMEM((count, SHARE * PIECE), f32), i...  42.6 us

profile of v5, /device:TPU:1, one launch (start us, length us, event | category | flops | bytes accessed | tf_op | source)
XLA Modules:
  0.0 43.2 jit_solution(18247463193749540630)
XLA Ops:
  0.0 42.6 %late_interaction.1 = f32[128,128]{1,0:T(8,128)S(1)} custom-call(s32[1,512]{1,0:T(1,128)} %bitcast.2, bf16[128,8,128]{2,1,0:T(8,128)(2,1)} %query_ref.1, s32[1,128]{1,0:T(1,128)} %bitcast.3, bf16[512,64,128]{2,1,0:T(8,128)(2,1)} %passages_ref.1), custom_call_target="tpu_custom_call" | custom-call | tf_op jit(solution)/shard_map/late_interaction/pallas_call | solution.py:280
  42.6 0.6 %copy.6 = f32[128,128]{1,0:T(8,128)} copy(f32[128,128]{1,0:T(8,128)S(1)} %late_interaction.1) | data formatting | bytes 131072

commit v6 on v4

--- a/solution.py
+++ b/solution.py
@@ -13,7 +13,7 @@
 HALF = PIECE * SHARE // 2
 ROWS = 8
 TILE = 256
-FAR = ((0, 16), (16, 16), (32, 32))
+FAR = ((0, 16), (16, 24), (40, 24))
 
 
 def body(

time: 43.2 us -> 43 us (level)
  no operation moved by 1% of the time
where the time goes in v6:
time: 43 us; the launch traced here: 42.9 us
  Pallas kernels  42.3 us (98%)
  local copies, waits for them, and re-layouts  0.63 us (1%)
    pallas_call x1, Pallas kernels, shards(): pl.pallas_call(body, out_shape=pltpu.VMEM((count, SHARE * PIECE), f32), i...  42.3 us

profile of v6, /device:TPU:1, one launch (start us, length us, event | category | flops | bytes accessed | tf_op | source)
XLA Modules:
  0.0 42.9 jit_solution(2619851989138319085)
XLA Ops:
  0.0 42.3 %late_interaction.1 = f32[128,128]{1,0:T(8,128)S(1)} custom-call(s32[1,512]{1,0:T(1,128)} %bitcast.2, bf16[128,8,128]{2,1,0:T(8,128)(2,1)} %query_ref.1, s32[1,128]{1,0:T(1,128)} %bitcast.3, bf16[512,64,128]{2,1,0:T(8,128)(2,1)} %passages_ref.1), custom_call_target="tpu_custom_call" | custom-call | tf_op jit(solution)/shard_map/late_interaction/pallas_call | solution.py:275
  42.3 0.6 %copy.6 = f32[128,128]{1,0:T(8,128)} copy(f32[128,128]{1,0:T(8,128)S(1)} %late_interaction.1) | data formatting | bytes 131072
